TPU v7x, 32 devices: a whole 2x2x4 slice. The times are simulated.
32 devices in a mesh: dp: 4 (over x, core), vocab: 8 (over z, y).
Axes of the slice: x: 2, y: 2, z: 4, core: 2. Of those that a mesh axis runs over, the one named last changes fastest.
Arguments:
- policy_hidden: bfloat16 [512, 4096], P('dp'), may hold values from -84 to 84
- policy_weight: bfloat16 [4096, 65536], P('dp', 'vocab'), may hold values from -0.09375 to 0.09375
- reference_hidden: bfloat16 [512, 4096], P(('dp', 'vocab')), may hold values from -84 to 84
- reference_weight: bfloat16 [4096, 65536], P(None, ('dp', 'vocab')), may hold values from -0.09375 to 0.09375
- targets: int32 [512], replicated, may hold values from 0 to 65535
- response_mask: int32 [512], replicated, may hold values 0 or 1
- pair_index: int32 [16], replicated, may hold values from 0 to 15, each once
Outputs:
- hidden_grad: bfloat16 [512, 4096], P('vocab', 'dp')
- weight_grad: bfloat16 [4096, 65536], P('dp', 'vocab')
- total_loss: float32 [], replicated
Inputs may be any that keep to these rules, and one draw needn't show every extreme that they name: `pair_index`: each number of 0 to 15 once; entries 2p and 2p + 1 are the chosen and the rejected sequence of pair p.
All inputs are finite; a program needn't handle non-finite values.
Results may differ from a plain program's by a relative error of at most 0.005.
The roundings to bfloat16 on the way count: a program that leaves them out, or rounds other values in their place, can miss the bound.
Values may be sent and summed in bfloat16 or wider, within the bound.
A program may use at most 128 MiB of HBM per device.

v0:
```python
import jax
import jax.numpy as jnp
from jax import lax
from jax.sharding import PartitionSpec as P

SEQ_LEN = 32
beta = 0.1
loss_scale = 4096.0


def pair_terms(log_ratio, pair_index):
    chosen = pair_index[0::2]
    rejected = pair_index[1::2]
    margin = beta * (log_ratio[chosen] - log_ratio[rejected])
    pair_count = chosen.shape[0]
    total_loss = jnp.sum(jax.nn.softplus(-margin)) / pair_count
    weight = -beta * loss_scale * jax.nn.sigmoid(-margin) / pair_count
    numbers = jnp.arange(log_ratio.shape[0], dtype=jnp.int32)[:, None]
    factor = jnp.sum(
        jnp.where(numbers == chosen[None, :], weight[None, :], 0.0)
        - jnp.where(numbers == rejected[None, :], weight[None, :], 0.0),
        axis=1,
    )
    return (total_loss, factor)


def local_pick(logits, targets, offset, axis):
    column_ids = lax.broadcasted_iota(jnp.int32, logits.shape, axis)
    shifted = targets - offset
    wanted = shifted[:, None]
    return jnp.sum(jnp.where(column_ids == wanted, logits, 0.0), axis=axis)


def local(
    policy_hidden,
    policy_weight,
    reference_hidden,
    reference_weight,
    targets,
    response_mask,
    pair_index,
):
    data_index = lax.axis_index("dp")
    vocab_index = lax.axis_index("vocab")
    vocab_devices = lax.axis_size("vocab")
    local_tokens = policy_hidden.shape[0]
    policy_width = policy_weight.shape[1]
    reference_width = reference_weight.shape[1]
    active = response_mask.astype(jnp.float32)
    columns = lax.all_to_all(policy_hidden, "dp", split_axis=1, concat_axis=0, tiled=True)
    reference_logits = jnp.dot(
        lax.all_gather(reference_hidden, ("dp", "vocab"), axis=0, tiled=True),
        reference_weight,
        preferred_element_type=jnp.float32,
    )
    reference_offset = (data_index * vocab_devices + vocab_index) * reference_width
    reference_top = jnp.max(reference_logits, axis=1)
    reference_pick = local_pick(reference_logits, targets, reference_offset, 1)
    policy_logits = lax.psum_scatter(
        jnp.dot(columns, policy_weight, preferred_element_type=jnp.float32),
        "dp",
        scatter_dimension=0,
        tiled=True,
    )
    own_targets = lax.dynamic_slice_in_dim(targets, data_index * local_tokens, local_tokens, 0)
    policy_offset = vocab_index * policy_width
    policy_pick = local_pick(policy_logits, own_targets, policy_offset, 1)
    policy_max = lax.pmax(jnp.max(policy_logits, axis=1), "vocab")
    policy_sum, policy_picked = lax.psum(
        (jnp.sum(jnp.exp(policy_logits - policy_max[:, None]), axis=1), policy_pick), "vocab"
    )
    policy_total = policy_max + jnp.log(policy_sum)
    reference_max = lax.pmax(reference_top, ("dp", "vocab"))
    reference_sum, reference_picked = lax.psum(
        (jnp.sum(jnp.exp(reference_logits - reference_max[:, None]), axis=1), reference_pick),
        ("dp", "vocab"),
    )
    reference_logp = reference_picked - reference_max - jnp.log(reference_sum)
    own_reference = lax.dynamic_slice_in_dim(
        reference_logp, data_index * local_tokens, local_tokens, 0
    )
    own_active = lax.dynamic_slice_in_dim(active, data_index * local_tokens, local_tokens, 0)
    own_ratio = jnp.sum(
        (own_active * (policy_picked - policy_total - own_reference)).reshape(-1, SEQ_LEN), axis=1
    )
    log_ratio = lax.all_gather(own_ratio, "dp", axis=0, tiled=True)
    total_loss, factor = pair_terms(log_ratio, pair_index)
    token_scale = lax.dynamic_slice_in_dim(
        active * jnp.repeat(factor, SEQ_LEN), data_index * local_tokens, local_tokens, 0
    )
    column_ids = lax.broadcasted_iota(jnp.int32, policy_logits.shape, 1)
    onehot = (column_ids == (own_targets - policy_offset)[:, None]).astype(jnp.float32)
    logit_grad = (
        token_scale[:, None] * (onehot - jnp.exp(policy_logits - policy_total[:, None]))
    ).astype(jnp.bfloat16)
    segment = lax.all_gather(logit_grad, "dp", axis=0, tiled=True)
    weight_grad = lax.dot_general(
        columns, segment, (((0,), (0,)), ((), ())), preferred_element_type=jnp.float32
    )
    hidden_piece = lax.dot_general(
        segment, policy_weight, (((1,), (1,)), ((), ())), preferred_element_type=jnp.float32
    )
    weight_grad, hidden_part = (weight_grad, hidden_piece)
    hidden_grad = lax.psum_scatter(hidden_part, "vocab", scatter_dimension=0, tiled=True)
    return (hidden_grad.astype(jnp.bfloat16), weight_grad.astype(jnp.bfloat16), total_loss)


def solution(mesh):
    placed = (
        P("dp", None),
        P("dp", "vocab"),
        P(("dp", "vocab"), None),
        P(None, ("dp", "vocab")),
        P(),
        P(),
        P(),
    )
    return jax.shard_map(
        local,
        mesh=mesh,
        in_specs=placed,
        out_specs=(P("vocab", "dp"), P("dp", "vocab"), P()),
        check_vma=False,
    )
```

profile of v0, /device:TPU:0, one launch (start us, length us, event | category | flops | bytes accessed | tf_op | source)
XLA Modules:
  0.0 385.9 jit_solution(17941225385931187928)
XLA Ops:
  8.0 0.0 all-gather.3.cloned.1.call-start
  8.0 0.7 all-gather.3.cloned.1.call-update
  8.7 0.0 reduce-scatter.3.cloned.1.call-start
  8.8 1.6 copy.15
  10.4 19.4 %all_to_all.19 = bf16[128,4,1024]{0,2,1:T(8,128)(2,1)S(1)} all-to-all(bf16[128,4,1024]{0,2,1:T(8,128)(2,1)S(1)} %bitcast.15), channel_id=1, replica_groups=mesh['dp'=4,'vocab'=8] {'dp'}, dimensions={1} | all-to-all | bytes 2097152 | tf_op jit(solution)/shard_map/all_to_all | solution.py:50
  29.8 0.5 copy.16
  30.4 15.8 %fusion.2 = f32[512,8192]{1,0:T(8,128)} fusion(bf16[512,1024]{1,0:T(8,128)(2,1)S(1)} %bitcast.16, bf16[1024,8192]{1,0:T(8,128)(2,1)} %param.8), kind=kOutput, calls=%fused_computation.28 | convolution fusion | flops 8589934592 | bytes 34603008 | tf_op jit(solution)/shard_map/dot_general | solution.py:60
  46.2 0.0 reduce-scatter.3.cloned.1.call-update
  46.2 0.0 all-gather.5.cloned.1.call-start
  46.3 0.6 copy-done.2
  46.8 0.1 slice.7
  46.9 0.1 slice.6
  47.0 0.0 copy-done
  47.1 0.6 dynamic-slice
  48.3 0.0 copy-done.1
  48.3 0.1 dynamic-slice_subtract_fusion
  48.4 28.4 %all-gather.3.cloned.1.call-done = bf16[512,4096]{1,0:T(8,128)(2,1)} async-done(((bf16[16,4096]{1,0:T(8,128)(2,1)}), bf16[512,4096]{1,0:T(8,128)(2,1)}) %all-gather.3.cloned.1.call-update) | async-done | bytes 4194320 | tf_op jit(solution)/shard_map/all_gather | solution.py:52
  76.8 15.7 %fusion.1 = (f32[512]{0:T(512)S(1)}, f32[512,2048]{1,0:T(8,128)}) fusion(bf16[512,4096]{1,0:T(8,128)(2,1)} %all-gather.3.cloned.1.call-done, bf16[4096,2048]{1,0:T(8,128)(2,1)} %param.10), kind=kOutput, calls=%fused_computation.27 | convolution fusion | flops 8590983168 | bytes 25167872 | tf_op jit(solution)/shard_map/dot_general | solution.py:51
  92.5 40.3 %pmax.15 = f32[512]{0:T(512)S(1)} all-reduce(f32[512]{0:T(512)S(1)} %get-tuple-element.27), channel_id=1, replica_groups=mesh['dp'=4,'vocab'=8] {'dp','vocab'}, use_global_device_ids=true, to_apply=%region_10.11 | all-reduce | flops 512 | bytes 4096 | tf_op jit(solution)/shard_map/pmax | solution.py:73
  132.8 3.6 select_reduce_fusion
  136.5 41.4 %all-reduce.1 = (f32[512]{0:T(512)S(1)}, f32[512]{0:T(512)S(1)}) all-reduce(f32[512]{0:T(512)S(1)} %get-tuple-element.18, f32[512]{0:T(512)S(1)} %get-tuple-element.17), channel_id=1, replica_groups=mesh['dp'=4,'vocab'=8] {'dp','vocab'}, use_global_device_ids=true, to_apply=%region_12.13 | all-reduce | flops 1024 | bytes 8192 | tf_op jit(solution)/shard_map/psum | solution.py:74
  177.9 0.0 reduce-scatter.3.cloned.1.call-done
  177.9 2.5 reduce_max.18
  180.3 20.9 %pmax.14 = f32[128]{0:T(128)S(1)} all-reduce(f32[128]{0:T(128)S(1)} %reduce_max.18), channel_id=1, replica_groups=mesh['dp'=4,'vocab'=8] {'vocab'}, use_global_device_ids=true, to_apply=%region_4.5 | all-reduce | flops 128 | bytes 1024 | tf_op jit(solution)/shard_map/pmax | solution.py:68
  201.2 3.4 select_reduce_fusion.1
  204.6 17.1 %all-reduce.2 = (f32[128]{0:T(128)S(1)}, f32[128]{0:T(128)S(1)}) all-reduce(f32[128]{0:T(128)S(1)} %get-tuple-element.16, f32[128]{0:T(128)S(1)} %get-tuple-element.15), channel_id=1, replica_groups=mesh['dp'=4,'vocab'=8] {'vocab'}, use_global_device_ids=true, to_apply=%region_6.7 | all-reduce | flops 256 | bytes 2048 | tf_op jit(solution)/shard_map/psum | solution.py:69
  221.8 0.1 subtract_multiply_fusion.1
  221.8 0.1 reshape.33
  221.9 0.1 reduce_sum.67
  222.1 0.2 dynamic-update-slice
  222.3 5.6 %all-reduce = f32[16]{0:T(128)S(1)} all-reduce(f32[16]{0:T(128)S(1)} %dynamic-update-slice), channel_id=1, replica_groups=mesh['dp'=4,'vocab'=8] {'dp'}, use_global_device_ids=true, to_apply=%add | all-reduce | flops 16 | bytes 128
  227.9 0.6 gather_fusion
  228.6 0.6 gather_fusion.1
  229.2 0.6 fusion
  229.8 0.1 subtract_reduce_fusion
  229.9 0.1 broadcast_in_dim.51
  230.0 0.1 reshape.34
  230.1 0.1 dynamic_slice.15
  230.2 4.7 %multiply_convert_fusion = bf16[128,8192]{1,0:T(8,128)(2,1)} fusion(f32[128,8192]{1,0:T(8,128)} %reduce-scatter.3.cloned.1.call-done, f32[128]{0:T(128)S(1)} %get-tuple-element.24, f32[128]{0:T(128)S(1)} %dynamic_slice.15, s32[128]{0:T(128)S(1)} %dynamic-slice_subtract_fusion), kind=kLoop, calls=%fused_computation.3 | loop fusion | flops 6291456 | bytes 6292992 | tf_op jit(solution)/shard_map/convert_element_type | solution.py:95
  234.9 0.0 all-gather.5.cloned.1.call-update
  234.9 0.0 reduce-scatter.5.cloned.1.call-start
  235.0 56.3 %all-gather.5.cloned.1.call-done = bf16[512,8192]{1,0:T(8,128)(2,1)} async-done(((bf16[128,8192]{1,0:T(8,128)(2,1)}), bf16[512,8192]{1,0:T(8,128)(2,1)}) %all-gather.5.cloned.1.call-update) | async-done | bytes 8388624 | tf_op jit(solution)/shard_map/all_gather | solution.py:96
  291.2 15.9 %fusion.3 = f32[512,1024]{1,0:T(8,128)} fusion(bf16[512,8192]{1,0:T(8,128)(2,1)} %all-gather.5.cloned.1.call-done, bf16[1024,8192]{1,0:T(8,128)(2,1)} %param.8), kind=kOutput, calls=%fused_computation.29 | convolution fusion | flops 8589934592 | bytes 27262976 | tf_op jit(solution)/shard_map/dot_general | solution.py:100
  307.1 0.0 reduce-scatter.5.cloned.1.call-update
  307.8 15.9 %convert_bitcast_fusion = bf16[1024,8192]{0,1:T(8,128)(2,1)} fusion(bf16[512,8192]{1,0:T(8,128)(2,1)} %all-gather.5.cloned.1.call-done, bf16[512,1024]{1,0:T(8,128)(2,1)S(1)} %bitcast.17), kind=kOutput, calls=%fused_computation.2 | convolution fusion | flops 8598323200 | bytes 26214400 | tf_op jit(solution)/shard_map/dot_general | solution.py:97
  323.7 21.3 %copy.17 = bf16[1024,8192]{1,0:T(8,128)(2,1)} copy(bf16[1024,8192]{0,1:T(8,128)(2,1)} %convert_bitcast_fusion) | data formatting | bytes 33554432
  345.0 30.7 %reduce-scatter.5.cloned.1.call-done = f32[64,1024]{1,0:T(8,128)} async-done(((f32[512,1024]{1,0:T(8,128)}), f32[64,1024]{1,0:T(8,128)}) %reduce-scatter.5.cloned.1.call-update) | async-done | bytes 262160 | tf_op jit(solution)/shard_map/reduce_scatter | solution.py:104
  375.8 1.6 convert_element_type.21
  (14 shorter events, 0.1 us)
Async XLA Ops:
  8.0 68.8 %all-gather.3.cloned.1.call-start = ((), (), s32[]{:S(2)}) async-start(), calls=%async_computation.4 | async-start | bytes 4325376 | tf_op jit(solution)/shard_map/all_gather | solution.py:52
  8.7 169.1 %reduce-scatter.3.cloned.1.call-start = ((), (), s32[]{:S(2)}) async-start(), calls=%async_computation.3 | async-start | bytes 20971520 | tf_op jit(solution)/shard_map/reduce_scatter | solution.py:59
  46.2 0.7 copy-start.2
  46.2 0.8 copy-start
  46.2 0.9 copy-start.3
  46.2 2.1 copy-start.1
  46.2 245.0 %all-gather.5.cloned.1.call-start = ((), (), s32[]{:S(2)}) async-start(), calls=%async_computation.5 | async-start | bytes 10485760 | tf_op jit(solution)/shard_map/all_gather | solution.py:96
  234.9 140.8 %reduce-scatter.5.cloned.1.call-start = ((), (), s32[]{:S(2)}) async-start(), calls=%async_computation.6 | async-start | bytes 2359296 | tf_op jit(solution)/shard_map/reduce_scatter | solution.py:104
Sparse Core Ops, SparseCore 0:
  11.9 64.9 all-gather.2
  307.3 68.4 reduce-scatter.4
Sparse Core Ops, SparseCore 1:
  46.3 128.4 reduce-scatter.2
  235.0 56.2 all-gather.4
where the time goes:
time: 387 us; the launch traced here: 386 us
  blocking collectives  145 us (37%)
  waiting for transfers between devices  116 us (30%)
  matrix products  63.3 us (16%)
  local copies, waits for them, and re-layouts  26.6 us (7%)
  between operations  18 us (5%)
  other arithmetic  16.9 us (4%)
    all_gather x1, waiting for transfers between devices, local(): segment = lax.all_gather(logit_grad, 'dp', axis=0, tiled=True)  56.3 us
    psum x1, blocking collectives, local(): lax.psum((jnp.sum(jnp.exp(reference_logits - reference_max[:, None]), axi...  41.4 us
    pmax x1, blocking collectives, local(): reference_max = lax.pmax(reference_top, ('dp', 'vocab'))  40.3 us
    reduce_scatter x1, waiting for transfers between devices, local(): lax.psum_scatter(hidden_part, 'vocab', scatter_dimension=0, tiled=True)  30.7 us
    all_gather x1, waiting for transfers between devices, local(): lax.all_gather(reference_hidden, ('dp', 'vocab'), axis=0, tiled=True)  28.4 us
    unnamed x13, local copies, waits for them, and re-layouts  24.3 us
    pmax x1, blocking collectives, local(): policy_max = lax.pmax(jnp.max(policy_logits, axis=1), 'vocab')  20.9 us
    all_to_all x1, blocking collectives, local(): lax.all_to_all(policy_hidden, 'dp', split_axis=1, concat_axis=0, tiled=True)  19.4 us
  transfers between devices with their start and end apart: 4, of which 3 were waited for; matrix products, arithmetic and copies ran while one was open for 20% of the time, Pallas kernels for 0%

commit v1 on v0

--- a/solution.py
+++ b/solution.py
@@ -6,6 +6,27 @@
 SEQ_LEN = 32
 beta = 0.1
 loss_scale = 4096.0
+
+
+def ring_gather(shard, axis, dim):
+    devices, position, rows = (lax.axis_size(axis), lax.axis_index(axis), shard.shape[dim])
+    upward = [(i, (i + 1) % devices) for i in range(devices)]
+    left = [(i, (i - 1) % devices) for i in range(devices)]
+    out = jnp.zeros((*shard.shape[:dim], devices * rows, *shard.shape[dim + 1 :]), shard.dtype)
+    out = lax.dynamic_update_slice_in_dim(out, shard, position * rows, axis=dim)
+    from_left = from_right = shard
+    halfway = devices // 2
+    for turn in range(1, halfway + 1):
+        from_left = lax.ppermute(from_left, axis, upward)
+        out = lax.dynamic_update_slice_in_dim(
+            out, from_left, (position - turn) % devices * rows, axis=dim
+        )
+        if turn < devices - halfway:
+            from_right = lax.ppermute(from_right, axis, left)
+            out = lax.dynamic_update_slice_in_dim(
+                out, from_right, (position + turn) % devices * rows, axis=dim
+            )
+    return out
 
 
 def pair_terms(log_ratio, pair_index):
@@ -93,7 +114,7 @@
     logit_grad = (
         token_scale[:, None] * (onehot - jnp.exp(policy_logits - policy_total[:, None]))
     ).astype(jnp.bfloat16)
-    segment = lax.all_gather(logit_grad, "dp", axis=0, tiled=True)
+    segment = ring_gather(logit_grad, "dp", 0)
     weight_grad = lax.dot_general(
         columns, segment, (((0,), (0,)), ((), ())), preferred_element_type=jnp.float32
     )

time: 387 us -> 407 us (1.052)
  local copies, waits for them, and re-layouts: 26.6 us -> 41.5 us
  waiting for transfers between devices: 116 us -> 122 us
    ppermute x0 -> x3, waiting for transfers between devices: none -> 64.8 us  [the longest x2 64.8 us: ring_gather(): from_left = lax.ppermute(from_left, axis, upward)]
    all_gather x1 -> x0, waiting for transfers between devices: 56.3 us -> none  [local(): segment = lax.all_gather(logit_grad, 'dp', axis=0, tiled=True)]
    dynamic_update_slice x0 -> x3, local copies, waits for them, and re-layouts: none -> 9.29 us  [the longest x2 6.19 us: ring_gather(): lax.dynamic_update_slice_in_dim(out, from_left, (position - turn) % devic...]
    convert_element_type x1 -> x0, other arithmetic: 4.73 us -> none  [local(): logit_grad = (token_scale[:, None] * (onehot - jnp.exp(policy_logits - po...]
    unnamed x13 -> x17, local copies, waits for them, and re-layouts: 24.3 us -> 28.9 us
  transfers between devices with their start and end apart: 4 -> 6, of which waited for: 3 -> 4; matrix products, arithmetic and copies ran while one was open for 20% -> 20% of each run, Pallas kernels for 0% -> 0%
where the time goes in v1:
time: 407 us; the launch traced here: 405 us
  blocking collectives  145 us (36%)
  waiting for transfers between devices  122 us (30%)
  matrix products  63.3 us (16%)
  local copies, waits for them, and re-layouts  41.5 us (10%)
  between operations  18 us (4%)
  other arithmetic  13.6 us (3%)
    ppermute x2, waiting for transfers between devices, ring_gather(): from_left = lax.ppermute(from_left, axis, upward)  64.8 us
    psum x1, blocking collectives, local(): lax.psum((jnp.sum(jnp.exp(reference_logits - reference_max[:, None]), axi...  41.4 us
    pmax x1, blocking collectives, local(): reference_max = lax.pmax(reference_top, ('dp', 'vocab'))  40.3 us
    unnamed x17, local copies, waits for them, and re-layouts  28.9 us
    reduce_scatter x1, waiting for transfers between devices, local(): lax.psum_scatter(hidden_part, 'vocab', scatter_dimension=0, tiled=True)  28.5 us
    all_gather x1, waiting for transfers between devices, local(): lax.all_gather(reference_hidden, ('dp', 'vocab'), axis=0, tiled=True)  28.4 us
    pmax x1, blocking collectives, local(): policy_max = lax.pmax(jnp.max(policy_logits, axis=1), 'vocab')  20.8 us
    all_to_all x1, blocking collectives, local(): lax.all_to_all(policy_hidden, 'dp', split_axis=1, concat_axis=0, tiled=True)  19.4 us
  transfers between devices with their start and end apart: 6, of which 4 were waited for; matrix products, arithmetic and copies ran while one was open for 20% of the time, Pallas kernels for 0%

profile of v1, /device:TPU:0, one launch (start us, length us, event | category | flops | bytes accessed | tf_op | source)
XLA Modules:
  0.0 405.4 jit_solution(17034184875286300246)
XLA Ops:
  8.0 0.7 all-gather.2.cloned.1.call-update
  8.7 0.0 reduce-scatter.3.cloned.1.call-start
  8.8 1.6 copy.15
  10.4 19.4 %all_to_all.19 = bf16[128,4,1024]{0,2,1:T(8,128)(2,1)S(1)} all-to-all(bf16[128,4,1024]{0,2,1:T(8,128)(2,1)S(1)} %bitcast.15), channel_id=1, replica_groups=mesh['dp'=4,'vocab'=8] {'dp'}, dimensions={1} | all-to-all | bytes 2097152 | tf_op jit(solution)/shard_map/all_to_all | solution.py:71
  29.8 0.5 copy.16
  30.3 15.8 %fusion.2 = f32[512,8192]{1,0:T(8,128)} fusion(bf16[512,1024]{1,0:T(8,128)(2,1)S(1)} %bitcast.16, bf16[1024,8192]{1,0:T(8,128)(2,1)} %param.8), kind=kOutput, calls=%fused_computation.32 | convolution fusion | flops 8589934592 | bytes 34603008 | tf_op jit(solution)/shard_map/dot_general | solution.py:81
  46.2 0.0 reduce-scatter.5.cloned.1.call-start
  46.3 0.6 copy-done.4
  46.8 0.1 slice.7
  46.9 0.1 slice.6
  47.1 0.6 dynamic-slice
  48.3 0.1 dynamic-slice_subtract_fusion
  48.4 28.4 %all-gather.2.cloned.1.call-done = bf16[512,4096]{1,0:T(8,128)(2,1)} async-done(((bf16[16,4096]{1,0:T(8,128)(2,1)}), bf16[512,4096]{1,0:T(8,128)(2,1)}) %all-gather.2.cloned.1.call-update) | async-done | bytes 4194320 | tf_op jit(solution)/shard_map/all_gather | solution.py:73
  76.8 15.7 %fusion.1 = (f32[512]{0:T(512)S(1)}, f32[512,2048]{1,0:T(8,128)}) fusion(bf16[512,4096]{1,0:T(8,128)(2,1)} %all-gather.2.cloned.1.call-done, bf16[4096,2048]{1,0:T(8,128)(2,1)} %param.10), kind=kOutput, calls=%fused_computation.31 | convolution fusion | flops 8590983168 | bytes 25167872 | tf_op jit(solution)/shard_map/dot_general | solution.py:72
  92.5 40.3 %pmax.15 = f32[512]{0:T(512)S(1)} all-reduce(f32[512]{0:T(512)S(1)} %get-tuple-element.29), channel_id=1, replica_groups=mesh['dp'=4,'vocab'=8] {'dp','vocab'}, use_global_device_ids=true, to_apply=%region_10.11 | all-reduce | flops 512 | bytes 4096 | tf_op jit(solution)/shard_map/pmax | solution.py:94
  132.8 3.6 select_reduce_fusion
  136.5 41.4 %all-reduce.1 = (f32[512]{0:T(512)S(1)}, f32[512]{0:T(512)S(1)}) all-reduce(f32[512]{0:T(512)S(1)} %get-tuple-element.18, f32[512]{0:T(512)S(1)} %get-tuple-element.17), channel_id=1, replica_groups=mesh['dp'=4,'vocab'=8] {'dp','vocab'}, use_global_device_ids=true, to_apply=%region_12.13 | all-reduce | flops 1024 | bytes 8192 | tf_op jit(solution)/shard_map/psum | solution.py:95
  177.9 2.5 reduce_max.18
  180.3 20.8 %pmax.14 = f32[128]{0:T(128)S(1)} all-reduce(f32[128]{0:T(128)S(1)} %reduce_max.18), channel_id=1, replica_groups=mesh['dp'=4,'vocab'=8] {'vocab'}, use_global_device_ids=true, to_apply=%region_4.5 | all-reduce | flops 128 | bytes 1024 | tf_op jit(solution)/shard_map/pmax | solution.py:89
  201.2 3.4 select_reduce_fusion.1
  204.6 17.1 %all-reduce.2 = (f32[128]{0:T(128)S(1)}, f32[128]{0:T(128)S(1)}) all-reduce(f32[128]{0:T(128)S(1)} %get-tuple-element.16, f32[128]{0:T(128)S(1)} %get-tuple-element.15), channel_id=1, replica_groups=mesh['dp'=4,'vocab'=8] {'vocab'}, use_global_device_ids=true, to_apply=%region_6.7 | all-reduce | flops 256 | bytes 2048 | tf_op jit(solution)/shard_map/psum | solution.py:90
  221.8 0.1 subtract_multiply_fusion.1
  221.8 0.1 reshape.33
  221.9 0.1 reduce_sum.67
  222.0 0.2 dynamic-update-slice
  222.3 5.6 %all-reduce = f32[16]{0:T(128)S(1)} all-reduce(f32[16]{0:T(128)S(1)} %dynamic-update-slice), channel_id=1, replica_groups=mesh['dp'=4,'vocab'=8] {'dp'}, use_global_device_ids=true, to_apply=%add | all-reduce | flops 16 | bytes 128
  227.9 0.6 gather_fusion
  228.6 0.6 gather_fusion.1
  229.2 0.6 fusion
  229.8 0.1 subtract_reduce_fusion
  229.9 0.1 broadcast_in_dim.55
  230.0 0.1 reshape.34
  230.1 0.1 dynamic_slice.15
  230.2 1.0 broadcast_in_dim.48
  231.2 1.2 copy-done
  232.4 1.4 constant_dynamic-update-slice_fusion.3
  233.7 3.4 copy-done.1
  237.1 1.7 collective-permute-start.1
  238.9 45.3 %collective-permute-done = bf16[128,8192]{1,0:T(8,128)(2,1)} collective-permute-done((bf16[128,8192]{1,0:T(8,128)(2,1)S(1)}, bf16[128,8192]{1,0:T(8,128)(2,1)}, u32[]{:S(2)}, u32[]{:S(2)}) %collective-permute-start) | collective-permute-done | bytes 2097184 | tf_op jit(solution)/shard_map/ppermute | solution.py:20
  284.1 3.1 constant_dynamic-update-slice_fusion.2
  287.2 3.1 constant_dynamic-update-slice_fusion.1
  290.3 19.6 %collective-permute-done.2 = bf16[128,8192]{1,0:T(8,128)(2,1)} collective-permute-done((bf16[128,8192]{1,0:T(8,128)(2,1)}, bf16[128,8192]{1,0:T(8,128)(2,1)}, u32[]{:S(2)}, u32[]{:S(2)}) %collective-permute-start.2) | collective-permute-done | bytes 2097184 | tf_op jit(solution)/shard_map/ppermute | solution.py:20
  309.9 3.1 constant_dynamic-update-slice_fusion
  313.0 15.8 %fusion.3 = f32[512,1024]{1,0:T(8,128)} fusion(bf16[512,8192]{1,0:T(8,128)(2,1)} %constant_dynamic-update-slice_fusion, bf16[1024,8192]{1,0:T(8,128)(2,1)} %param.8), kind=kOutput, calls=%fused_computation.33 | convolution fusion | flops 8589934592 | bytes 27262976 | tf_op jit(solution)/shard_map/dot_general | solution.py:121
  329.5 15.9 %convert_bitcast_fusion = bf16[1024,8192]{0,1:T(8,128)(2,1)} fusion(bf16[512,8192]{1,0:T(8,128)(2,1)} %constant_dynamic-update-slice_fusion, bf16[512,1024]{1,0:T(8,128)(2,1)S(1)} %bitcast.17), kind=kOutput, calls=%fused_computation.2 | convolution fusion | flops 8598323200 | bytes 26214400 | tf_op jit(solution)/shard_map/dot_general | solution.py:118
  345.4 21.3 %copy.17 = bf16[1024,8192]{1,0:T(8,128)(2,1)} copy(bf16[1024,8192]{0,1:T(8,128)(2,1)} %convert_bitcast_fusion) | data formatting | bytes 33554432
  366.7 28.5 %reduce-scatter.5.cloned.1.call-done = f32[64,1024]{1,0:T(8,128)} async-done(((f32[512,1024]{1,0:T(8,128)}), f32[64,1024]{1,0:T(8,128)}) %reduce-scatter.5.cloned.1.call-update) | async-done | bytes 262160 | tf_op jit(solution)/shard_map/reduce_scatter | solution.py:125
  395.2 1.6 convert_element_type.21
  (24 shorter events, 0.2 us)
Async XLA Ops:
  8.0 68.8 %all-gather.2.cloned.1.call-start = ((), (), s32[]{:S(2)}) async-start(), calls=%async_computation.4 | async-start | bytes 4325376 | tf_op jit(solution)/shard_map/all_gather | solution.py:73
  8.7 169.1 %reduce-scatter.3.cloned.1.call-start = ((), (), s32[]{:S(2)}) async-start(), calls=%async_computation.3 | async-start | bytes 20971520 | tf_op jit(solution)/shard_map/reduce_scatter | solution.py:80
  46.2 0.7 copy-start.4
  46.2 0.8 copy-start.2
  46.2 0.9 copy-start.5
  46.2 2.1 copy-start.3
  46.2 349.0 %reduce-scatter.5.cloned.1.call-start = ((), (), s32[]{:S(2)}) async-start(), calls=%async_computation.5 | async-start | bytes 2359296 | tf_op jit(solution)/shard_map/reduce_scatter | solution.py:125
  230.2 2.2 copy-start
  233.7 3.4 copy-start.1
  237.1 47.0 %collective-permute-start = (bf16[128,8192]{1,0:T(8,128)(2,1)S(1)}, bf16[128,8192]{1,0:T(8,128)(2,1)}, u32[]{:S(2)}, u32[]{:S(2)}) collective-permute-start(bf16[128,8192]{1,0:T(8,128)(2,1)S(1)} %get-tuple-element.24), channel_id=1, source_target_pairs={{0,8},{8,16},{16,24},{24,0},{1,9},{9,17},{17,25},{25,1},{2,10},{10... | collective-permute-start | bytes 6291464 | tf_op jit(solution)/shard_map/ppermute | solution.py:20
  237.1 50.1 %collective-permute-start.1 = (bf16[128,8192]{1,0:T(8,128)(2,1)S(1)}, bf16[128,8192]{1,0:T(8,128)(2,1)}, u32[]{:S(2)}, u32[]{:S(2)}) collective-permute-start(bf16[128,8192]{1,0:T(8,128)(2,1)S(1)} %get-tuple-element.24), channel_id=1, source_target_pairs={{0,24},{8,0},{16,8},{24,16},{1,25},{9,1},{17,9},{25,17},{2,26},{10... | collective-permute-start | bytes 6291464 | tf_op jit(solution)/shard_map/ppermute | solution.py:25
  284.1 25.8 %collective-permute-start.2 = (bf16[128,8192]{1,0:T(8,128)(2,1)}, bf16[128,8192]{1,0:T(8,128)(2,1)}, u32[]{:S(2)}, u32[]{:S(2)}) collective-permute-start(bf16[128,8192]{1,0:T(8,128)(2,1)} %collective-permute-done), channel_id=1, source_target_pairs={{0,8},{8,16},{16,24},{24,0},{1,9},{9,17},{17,25},{25,1},{2,10},{10... | collective-permute-start | bytes 6291464 | tf_op jit(solution)/shard_map/ppermute | solution.py:20
Sparse Core Ops, SparseCore 0:
  11.9 64.9 all-gather.1
  329.0 66.1 reduce-scatter.4
Sparse Core Ops, SparseCore 1:
  46.3 128.4 reduce-scatter.2
